TPU v7x, 32 devices: a whole 2x2x4 slice. The times are simulated.
32 devices in a mesh: rep: 4 (over x, y), dp: 8 (over z, core).
Axes of the slice: x: 2, y: 2, z: 4, core: 2. Of those that a mesh axis runs over, the one named last changes fastest.
Arguments:
- x: bfloat16 [32, 4096, 640], P(('rep', 'dp')), parts along dimension 0
- dy: bfloat16 [32, 4096, 640], P(('rep', 'dp')), parts along dimension 0
- w_gate: bfloat16 [2, 640, 2560], P(None, 'dp')
- w_up: bfloat16 [2, 640, 2560], P(None, 'dp')
- w_down: bfloat16 [2, 2560, 640], P(None, 'dp')
Outputs:
- output 1: bfloat16 [32, 4096, 640], P(('rep', 'dp')), parts along dimension 0
- output 2: bfloat16 [8, 640, 2560], P('rep', 'dp'), parts along dimension 0
- output 3: bfloat16 [8, 640, 2560], P('rep', 'dp'), parts along dimension 0
- output 4: bfloat16 [8, 2560, 640], P('rep', 'dp'), parts along dimension 0
There are 4 independent parts. A program takes and returns all parts, laid end to end along the dimension named above; an argument that names none is the same for every part.
All inputs are finite; a program needn't handle non-finite values.
Results may differ from a plain program's by a relative error of at most 0.018.
Values are sent between devices in bfloat16 or wider.
A program may use at most 2 GiB of HBM per device.

v0:
```python
import jax
import jax.numpy as jnp
from jax import lax

NAMES = ("w_gate", "w_up", "w_down")


def matmul(a, w):
    return jnp.dot(a, w, preferred_element_type=jnp.float32).astype(jnp.bfloat16)


def normed(h):
    wide = h.astype(jnp.float32)
    scale = lax.rsqrt(jnp.mean(wide**2, -1, keepdims=True) + 1e-6)
    return (wide * scale).astype(jnp.bfloat16)


def layer(h, w):
    a = normed(h)
    gate = jnp.dot(a, w["w_gate"], preferred_element_type=jnp.float32)
    up = jnp.dot(a, w["w_up"], preferred_element_type=jnp.float32)
    return h + matmul((jax.nn.silu(gate) * up).astype(jnp.bfloat16), w["w_down"])


def stack(weights, h):
    for number in range(weights["w_gate"].shape[0]):
        h = layer(h, {name: w[number] for name, w in weights.items()})
    return h


def solution(mesh):
    groups = mesh.shape["rep"]

    def step(x, dy, *weights):
        shape = x.shape
        x, dy = (t.reshape(groups, -1, *t.shape[1:]) for t in (x, dy))

        def of_a_group(x, dy):
            _, back = jax.vjp(stack, dict(zip(NAMES, weights, strict=True)), x)
            by_weights, by_x = back(dy)
            return (by_x, *(by_weights[name] for name in NAMES))

        by_x, *by_weights = jax.vmap(of_a_group)(x, dy)
        return (by_x.reshape(shape), *(t.reshape(-1, *t.shape[2:]) for t in by_weights))

    return step
```

profile of v0, /device:TPU:0, one launch (start us, length us, event | category | flops | bytes accessed | tf_op | source)
XLA Modules:
  0.0 1144.4 jit_solution(14524293897086556944)
XLA Ops:
  43.3 8.0 all-gather.30.cloned.1.call-done
  51.3 25.1 %fusion.239 = f32[4096,2560]{1,0:T(8,128)} fusion(bf16[1,640,2560]{2,1,0:T(8,128)(2,1)} %all-gather.30.cloned.1.call-done, bf16[1,4096,640]{2,1,0:T(8,128)(2,1)} %param.13, f32[4096]{0:T(1024)S(1)} %get-tuple-element.267), kind=kOutput, calls=%fused_computation.260 | convolution fusion | flops 13429637120 | bytes 50479104 | tf_op jit(solution)/vmap(jvp())/dot_general | solution.py:20
  76.5 14.6 %all-gather.32.cloned.1.call-done = bf16[1,640,2560]{2,1,0:T(8,128)(2,1)} async-done(((bf16[1,80,2560]{2,1,0:T(8,128)(2,1)}), bf16[1,640,2560]{2,1,0:T(8,128)(2,1)}) %all-gather.32.cloned.1.call-update) | async-done | bytes 3276816 | tf_op jit(solution)/vmap(jvp())/squeeze | solution.py:27
  91.1 39.2 %fusion.168 = (bf16[1,1,4096,2560]{3,2,1,0:T(8,128)(2,1)}, f32[4096,2560]{1,0:T(8,128)}) fusion(f32[4096,2560]{1,0:T(8,128)} %fusion.239, bf16[1,640,2560]{2,1,0:T(8,128)(2,1)} %all-gather.32.cloned.1.call-done, bf16[1,4096,640]{2,1,0:T(8,128)(2,1)} %param.13, f32[4096]{0:T(1024)S(1)} %get-tuple-element.267), kind=kOutput, calls=%fused_computation.195 | convolution fusion | flops 13492551680 | bytes 113393664 | tf_op jit(solution)/vmap(jvp())/dot_general | solution.py:21
  130.3 26.3 %copy.4 = bf16[1,1,4096,2560]{2,3,1,0:T(8,128)(2,1)} copy(bf16[1,1,4096,2560]{3,2,1,0:T(8,128)(2,1)} %get-tuple-element.268) | data formatting | bytes 41943040
  156.7 21.4 %fusion.182 = (f32[4096]{0:T(1024)S(1)}, bf16[1,1,4096,640]{2,3,1,0:T(8,128)(2,1)S(1)}) fusion(bf16[1,2560,640]{2,1,0:T(8,128)(2,1)} %all-gather.34.cloned.1.call-done, bf16[1,1,4096,2560]{3,2,1,0:T(8,128)(2,1)} %get-tuple-element.268, bf16[1,4096,640]{1,2,0:T(8,128)(2,1)} %copy.1), kind=kOutput, calls=%fused_computation.225 | convolution fusion | flops 13434875904 | bytes 34750464 | tf_op jit(solution)/vmap(jvp())/dot_general | solution.py:9
  183.9 22.4 %convolution_convert_fusion.1 = bf16[4096,2560]{1,0:T(8,128)(2,1)} fusion(bf16[1,4096,640]{2,1,0:T(8,128)(2,1)} %param.12, bf16[1,2560,640]{2,1,0:T(8,128)(2,1)} %all-gather.38.cloned.1.call-done), kind=kOutput, calls=%fused_computation.203 | convolution fusion | flops 13432258560 | bytes 29491200 | tf_op jit(solution)/vmap(transpose(jvp()))/dot_general | solution.py:9
  210.1 27.1 %fusion.224 = f32[4096,2560]{1,0:T(8,128)} fusion(bf16[1,1,4096,640]{2,3,1,0:T(8,128)(2,1)} %fusion.183, bf16[1,640,2560]{2,1,0:T(8,128)(2,1)} %all-gather.40.cloned.1.call-done), kind=kOutput, calls=%fused_computation.245 | convolution fusion | flops 13421772800 | bytes 50462720 | tf_op jit(solution)/vmap(jvp())/dot_general | solution.py:21
  237.2 12.5 %all-gather.36.cloned.1.call-done = bf16[1,640,2560]{2,1,0:T(8,128)(2,1)} async-done(((bf16[1,80,2560]{2,1,0:T(8,128)(2,1)}), bf16[1,640,2560]{2,1,0:T(8,128)(2,1)}) %all-gather.36.cloned.1.call-update) | async-done | bytes 3276816 | tf_op jit(solution)/vmap(jvp())/squeeze | solution.py:27
  249.7 61.0 %fusion.153 = (bf16[1,1,4096,2560]{3,2,1,0:T(8,128)(2,1)}, bf16[1,1,4096,2560]{3,2,1,0:T(8,128)(2,1)}, f32[4096,2560]{1,0:T(8,128)}) fusion(f32[4096,2560]{1,0:T(8,128)} %fusion.224, bf16[4096,2560]{1,0:T(8,128)(2,1)} %convolution_convert_fusion.1, bf16[1,640,2560]{2,1,0:T(8,128)(2,1)} %all-gather.36.cloned.1.call-done, bf16[1,1,4096,640]{2,3,1,0:T(8,128)(2,1)} %fusion.183), kind=kOutput, calls=%fused_computation.175 | convolution fusion | flops 13579059200 | bytes 155320320 | tf_op jit(solution)/vmap(jvp())/dot_general | solution.py:20
  310.7 34.5 %fusion.162 = bf16[1,1,4096,2560]{3,2,1,0:T(8,128)(2,1)} fusion(f32[4096,2560]{1,0:T(8,128)} %fusion.224, f32[4096,2560]{1,0:T(8,128)} %get-tuple-element.272), kind=kLoop, calls=%fused_computation.185 | loop fusion | flops 62914560 | bytes 104857600 | tf_op jit(solution)/vmap(jvp())/convert_element_type | solution.py:22
  345.1 26.8 %copy.2 = bf16[1,1,4096,2560]{2,3,1,0:T(8,128)(2,1)} copy(bf16[1,1,4096,2560]{3,2,1,0:T(8,128)(2,1)} %fusion.162) | data formatting | bytes 41943040
  372.0 85.5 %while.16 = (bf16[1,1,4096,2560]{2,3,1,0:T(8,128)(2,1)}, bf16[1,1,4096,640]{3,2,1,0:T(8,128)(2,1)}, f32[1,320,640]{2,1,0:T(8,128)S(1)}, f32[1,320,640]{2,1,0:T(8...) while((bf16[1,1,4096,2560]{2,3,1,0:T(8,128)(2,1)}, ...), condition=%wide.windowed_dot_general_cond_rs.4.clone, body=%wide.windowed_dot_general_body_rs.4.clone.sunk | while | flops 6733086720 | bytes 81920608 | solution.py:9
  385.8 8.5 collective-permute-done.16
  405.8 9.5 collective-permute-done.18
  458.9 20.6 %fusion.188 = bf16[4096,640]{0,1:T(8,128)(2,1)} fusion(bf16[1,1,4096,2560]{3,2,1,0:T(8,128)(2,1)} %get-tuple-element.628, bf16[1,640,2560]{2,1,0:T(8,128)(2,1)} %all-gather.40.cloned.1.call-done), kind=kOutput, calls=%fused_computation.229 | convolution fusion | flops 13421772800 | bytes 29491200 | tf_op jit(solution)/vmap(transpose(jvp()))/dot_general | solution.py:21
  479.5 23.4 %fusion.184 = (f32[4096]{0:T(1024)S(1)}, bf16[1,1,4096,640]{2,3,1,0:T(8,128)(2,1)}) fusion(bf16[1,1,4096,640]{2,3,1,0:T(8,128)(2,1)} %copy-done.12, bf16[4096,640]{0,1:T(8,128)(2,1)} %fusion.188, bf16[1,640,2560]{2,1,0:T(8,128)(2,1)} %all-gather.36.cloned.1.call-done, bf16[1,1,4096,2560]{3,2,1,0:T(8,128)(2,1)} %get-tuple-element.550), kind=kOutput, calls=%fused_computation.227 | convolution fusion | flops 13434875904 | bytes 39993344 | tf_op jit(solution)/vmap(transpose(jvp()))/dot_general | solution.py:20
  502.9 11.8 %fusion.220 = bf16[1,1,4096,640]{2,3,1,0:T(8,128)(2,1)} fusion(bf16[1,1,4096,640]{2,3,1,0:T(8,128)(2,1)} %copy-done.12, bf16[1,1,4096,640]{2,3,1,0:T(8,128)(2,1)} %get-tuple-element.274, f32[4096]{0:T(1024)S(1)} %bitcast.600, f32[4096]{0:T(1024)S(1)} %bitcast.595, bf16[1,4096,640]{1,2,0:T(8,128)(2,1)} %copy), kind=kLoop, calls=%fused_computation.241 | loop fusion | flops 18350080 | bytes 21004288 | tf_op jit(solution)/vmap(transpose(jvp()))/add_any | solution.py:13
  514.7 8.2 copy.5
  523.0 89.9 %while.17 = (bf16[1,1,4096,2560]{2,3,1,0:T(8,128)(2,1)}, bf16[1,1,4096,640]{3,2,1,0:T(8,128)(2,1)}, f32[1,320,640]{2,1,0:T(8,128)S(1)}, f32[1,320,640]{2,1,0:T(8...) while((bf16[1,1,4096,2560]{2,3,1,0:T(8,128)(2,1)}, ...), condition=%wide.windowed_dot_general_cond_rs.5.clone, body=%wide.windowed_dot_general_body_rs.5.clone.sunk | while | flops 6733086720 | bytes 81920608 | solution.py:9
  557.0 10.2 collective-permute-done.22
  603.3 8.5 collective-permute-done.22
  614.0 100.4 %while.14 = (bf16[1,1,4096,640]{2,3,1,0:T(8,128)(2,1)}, bf16[1,1,4096,2560]{3,2,1,0:T(8,128)(2,1)}, f32[1,80,2560]{2,1,0:T(8,128)S(1)}, f32[1,80,2560]{2,1,0:T(8...) while((bf16[1,1,4096,640]{2,3,1,0:T(8,128)(2,1)}, ...), condition=%wide.windowed_dot_general_cond_rs.2.clone, body=%wide.windowed_dot_general_body_rs.2.clone.sunk | while | flops 6717358080 | bytes 144835312 | solution.py:21
  622.2 9.4 fusion.321
  631.6 12.4 %collective-permute-done.8 = f32[1,80,2560]{2,1,0:T(8,128)S(1)} collective-permute-done((f32[1,80,2560]{2,1,0:T(8,128)}, f32[1,80,2560]{2,1,0:T(8,128)S(1)}, u32[]{:S(2)}, u32[]{:S(2)}) %collective-permute-start.8) | collective-permute-done | bytes 819232 | tf_op jit(solution)/vmap(transpose(jvp()))/dot_general | solution.py:21
  653.5 10.3 collective-permute-done.10
  675.5 9.4 fusion.321
  699.2 12.9 %collective-permute-done.10 = f32[1,80,2560]{2,1,0:T(8,128)S(1)} collective-permute-done((f32[1,80,2560]{2,1,0:T(8,128)}, f32[1,80,2560]{2,1,0:T(8,128)S(1)}, u32[]{:S(2)}, u32[]{:S(2)}) %collective-permute-start.10) | collective-permute-done | bytes 819232 | tf_op jit(solution)/vmap(transpose(jvp()))/dot_general | solution.py:21
  714.5 52.9 %fusion.155 = (bf16[1,1,4096,2560]{3,2,1,0:T(8,128)(2,1)}, bf16[1,1,4096,2560]{3,2,1,0:T(8,128)(2,1)}) fusion(f32[4096,2560]{1,0:T(8,128)} %fusion.239, f32[4096,2560]{1,0:T(8,128)} %get-tuple-element.269, bf16[1,2560,640]{2,1,0:T(8,128)(2,1)} %all-gather.34.cloned.1.call-done, bf16[1,1,4096,640]{2,3,1,0:T(8,128)(2,1)} %fusion.220), kind=kOutput, calls=%fused_computation.177 | convolution fusion | flops 13589544960 | bytes 134348800 | tf_op jit(solution)/vmap(transpose(jvp()))/dot_general | solution.py:9
  767.4 19.5 %fusion.194 = bf16[4096,640]{0,1:T(8,128)(2,1)} fusion(bf16[1,1,4096,2560]{3,2,1,0:T(8,128)(2,1)} %get-tuple-element.589, bf16[1,640,2560]{2,1,0:T(8,128)(2,1)S(1)} %copy-done.22), kind=kOutput, calls=%fused_computation.231 | convolution fusion | flops 13421772800 | bytes 29491200 | tf_op jit(solution)/vmap(transpose(jvp()))/dot_general | solution.py:21
  786.9 24.9 %fusion.181 = (bf16[1,1,4096,640]{2,3,1,0:T(8,128)(2,1)}, f32[4096]{0:T(1024)}, bf16[1,1,4096,640]{2,3,1,0:T(8,128)(2,1)}) fusion(bf16[1,4096,640]{1,2,0:T(8,128)(2,1)} %copy.1, f32[4096]{0:T(1024)S(1)} %bitcast.602, bf16[4096,640]{0,1:T(8,128)(2,1)} %fusion.194, bf16[1,640,2560]{2,1,0:T(8,128)(2,1)} %all-gather.30.cloned.1.call-done, ...), kind=kOutput, calls=%fused_computation.224 | convolution fusion | flops 13440118784 | bytes 45252608 | tf_op jit(solution)/vmap(transpose(jvp()))/dot_general | solution.py:20
  811.8 94.1 %while.15 = (bf16[1,1,4096,640]{2,3,1,0:T(8,128)(2,1)}, bf16[1,1,4096,2560]{3,2,1,0:T(8,128)(2,1)}, f32[1,80,2560]{2,1,0:T(8,128)S(1)}, f32[1,80,2560]{2,1,0:T(8...) while((bf16[1,1,4096,640]{2,3,1,0:T(8,128)(2,1)}, ...), condition=%wide.windowed_dot_general_cond_rs.3.clone, body=%wide.windowed_dot_general_body_rs.3.clone.sunk | while | flops 6717358080 | bytes 144835312 | solution.py:21
  820.0 9.4 fusion.329
  843.4 13.5 %collective-permute-done.14 = f32[1,80,2560]{2,1,0:T(8,128)S(1)} collective-permute-done((f32[1,80,2560]{2,1,0:T(8,128)}, f32[1,80,2560]{2,1,0:T(8,128)S(1)}, u32[]{:S(2)}, u32[]{:S(2)}) %collective-permute-start.14) | collective-permute-done | bytes 819232 | tf_op jit(solution)/vmap(transpose(jvp()))/dot_general | solution.py:21
  868.6 9.4 fusion.329
  892.1 11.5 %collective-permute-done.14 = f32[1,80,2560]{2,1,0:T(8,128)S(1)} collective-permute-done((f32[1,80,2560]{2,1,0:T(8,128)}, f32[1,80,2560]{2,1,0:T(8,128)S(1)}, u32[]{:S(2)}, u32[]{:S(2)}) %collective-permute-start.14) | collective-permute-done | bytes 819232 | tf_op jit(solution)/vmap(transpose(jvp()))/dot_general | solution.py:21
  906.7 94.0 %while.12 = (bf16[1,1,4096,640]{2,3,1,0:T(8,128)(2,1)}, bf16[1,1,4096,2560]{3,2,1,0:T(8,128)(2,1)}, f32[1,80,2560]{2,1,0:T(8,128)S(1)}, f32[1,80,2560]{2,1,0:T(8...) while((bf16[1,1,4096,640]{2,3,1,0:T(8,128)(2,1)}, ...), condition=%wide.windowed_dot_general_cond_rs.clone, body=%wide.windowed_dot_general_body_rs.clone.sunk | while | flops 6717358080 | bytes 144835312 | solution.py:20
  915.3 9.4 fusion.305
  939.6 11.9 %collective-permute-done.2 = f32[1,80,2560]{2,1,0:T(8,128)S(1)} collective-permute-done((f32[1,80,2560]{2,1,0:T(8,128)}, f32[1,80,2560]{2,1,0:T(8,128)S(1)}, u32[]{:S(2)}, u32[]{:S(2)}) %collective-permute-start.2) | collective-permute-done | bytes 819232 | tf_op jit(solution)/vmap(transpose(jvp()))/dot_general | solution.py:20
  963.2 9.4 fusion.305
  987.1 11.4 %collective-permute-done.2 = f32[1,80,2560]{2,1,0:T(8,128)S(1)} collective-permute-done((f32[1,80,2560]{2,1,0:T(8,128)}, f32[1,80,2560]{2,1,0:T(8,128)S(1)}, u32[]{:S(2)}, u32[]{:S(2)}) %collective-permute-start.2) | collective-permute-done | bytes 819232 | tf_op jit(solution)/vmap(transpose(jvp()))/dot_general | solution.py:20
  1000.7 92.9 %while.13 = (bf16[1,1,4096,640]{2,3,1,0:T(8,128)(2,1)}, bf16[1,1,4096,2560]{3,2,1,0:T(8,128)(2,1)}, f32[1,80,2560]{2,1,0:T(8,128)S(1)}, f32[1,80,2560]{2,1,0:T(8...) while((bf16[1,1,4096,640]{2,3,1,0:T(8,128)(2,1)}, ...), condition=%wide.windowed_dot_general_cond_rs.1.clone, body=%wide.windowed_dot_general_body_rs.1.clone.sunk | while | flops 6717358080 | bytes 144835312 | solution.py:20
  1009.1 9.4 fusion.313
  1032.8 11.3 collective-permute-done.6
  1055.9 9.4 fusion.313
  1079.8 11.6 %collective-permute-done.6 = f32[1,80,2560]{2,1,0:T(8,128)S(1)} collective-permute-done((f32[1,80,2560]{2,1,0:T(8,128)}, f32[1,80,2560]{2,1,0:T(8,128)S(1)}, u32[]{:S(2)}, u32[]{:S(2)}) %collective-permute-start.6) | collective-permute-done | bytes 819232 | tf_op jit(solution)/vmap(transpose(jvp()))/dot_general | solution.py:20
  1094.0 11.8 %fusion.219 = bf16[1,4096,640]{1,2,0:T(8,128)(2,1)} fusion(bf16[1,1,4096,640]{2,3,1,0:T(8,128)(2,1)} %fusion.220, bf16[1,1,4096,640]{2,3,1,0:T(8,128)(2,1)} %get-tuple-element.275, bf16[1,4096,640]{1,2,0:T(8,128)(2,1)} %copy.1, f32[4096]{0:T(1024)S(1)} %bitcast.601, f32[4096]{0:T(1024)S(1)} %bitcast.603), kind=kLoop, calls=%fused_computation.240 | loop fusion | flops 18350080 | bytes 21004288 | tf_op jit(solution)/reshape | solution.py:44
  1127.4 8.7 collective-permute-done.25
  (361 shorter events, 384.5 us)
Async XLA Ops:
  7.2 44.2 %all-gather.30.cloned.1.call-start = ((), (), s32[]{:S(2)}) async-start(), calls=%async_computation | async-start | bytes 3686400 | tf_op jit(solution)/vmap(jvp())/squeeze | solution.py:27
  9.3 81.8 %all-gather.32.cloned.1.call-start = ((), (), s32[]{:S(2)}) async-start(), calls=%async_computation.1 | async-start | bytes 3686400 | tf_op jit(solution)/vmap(jvp())/squeeze | solution.py:27
  11.5 145.2 %all-gather.34.cloned.1.call-start = ((), (), s32[]{:S(2)}) async-start(), calls=%async_computation.2 | async-start | bytes 3686400 | tf_op jit(solution)/vmap(jvp())/squeeze | solution.py:27
  13.7 170.3 %all-gather.38.cloned.1.call-start = ((), (), s32[]{:S(2)}) async-start(), calls=%async_computation.4 | async-start | bytes 3686400 | tf_op jit(solution)/vmap(jvp())/squeeze | solution.py:27
  14.3 195.8 %all-gather.40.cloned.1.call-start = ((), (), s32[]{:S(2)}) async-start(), calls=%async_computation.5 | async-start | bytes 3686400 | tf_op jit(solution)/vmap(jvp())/squeeze | solution.py:27
  14.9 234.8 %all-gather.36.cloned.1.call-start = ((), (), s32[]{:S(2)}) async-start(), calls=%async_computation.3 | async-start | bytes 3686400 | tf_op jit(solution)/vmap(jvp())/squeeze | solution.py:27
  372.1 22.2 %collective-permute-start.16 = (f32[1,320,640]{2,1,0:T(8,128)S(1)}, f32[1,320,640]{2,1,0:T(8,128)S(1)}, u32[]{:S(2)}, u32[]{:S(2)}) collective-permute-start(f32[1,320,640]{2,1,0:T(8,128)S(1)} %broadcast_select_fusion.32), channel_id=39, source_target_pairs={{0,1},{1,2},{2,3},{3,4},{4,5},{5,6},{6,7},{7,0},{8,9},{9,10},{10,1... | collective-permute-start | bytes 2457608 | tf_op jit(solution)/vmap(transpose(jvp()))/dot_general | solution.py:9
  372.4 21.9 %collective-permute-start.17 = (f32[1,320,640]{2,1,0:T(8,128)S(1)}, f32[1,320,640]{2,1,0:T(8,128)S(1)}, u32[]{:S(2)}, u32[]{:S(2)}) collective-permute-start(f32[1,320,640]{2,1,0:T(8,128)S(1)} %broadcast_select_fusion.33), channel_id=38, source_target_pairs={{0,7},{1,0},{2,1},{3,2},{4,3},{5,4},{6,5},{7,6},{8,15},{9,8},{10,9... | collective-permute-start | bytes 2457608 | tf_op jit(solution)/vmap(transpose(jvp()))/dot_general | solution.py:9
  394.5 20.8 %collective-permute-start.18 = (f32[1,320,640]{2,1,0:T(8,128)S(1)}, f32[1,320,640]{2,1,0:T(8,128)S(1)}, u32[]{:S(2)}, u32[]{:S(2)}) collective-permute-start(f32[1,320,640]{2,1,0:T(8,128)S(1)} %get-tuple-element.497), channel_id=41, source_target_pairs={{0,1},{1,2},{2,3},{3,4},{4,5},{5,6},{6,7},{7,0},{8,9},{9,10},{10,1... | collective-permute-start | bytes 2457608 | tf_op jit(solution)/vmap(transpose(jvp()))/dot_general | solution.py:9
  394.5 20.8 %collective-permute-start.19 = (f32[1,320,640]{2,1,0:T(8,128)S(1)}, f32[1,320,640]{2,1,0:T(8,128)S(1)}, u32[]{:S(2)}, u32[]{:S(2)}) collective-permute-start(f32[1,320,640]{2,1,0:T(8,128)S(1)} %get-tuple-element.498), channel_id=40, source_target_pairs={{0,7},{1,0},{2,1},{3,2},{4,3},{5,4},{6,5},{7,6},{8,15},{9,8},{10,9... | collective-permute-start | bytes 2457608 | tf_op jit(solution)/vmap(transpose(jvp()))/dot_general | solution.py:9
  417.6 19.9 %collective-permute-start.16 = (f32[1,320,640]{2,1,0:T(8,128)S(1)}, f32[1,320,640]{2,1,0:T(8,128)S(1)}, u32[]{:S(2)}, u32[]{:S(2)}) collective-permute-start(f32[1,320,640]{2,1,0:T(8,128)S(1)} %broadcast_select_fusion.32), channel_id=39, source_target_pairs={{0,1},{1,2},{2,3},{3,4},{4,5},{5,6},{6,7},{7,0},{8,9},{9,10},{10,1... | collective-permute-start | bytes 2457608 | tf_op jit(solution)/vmap(transpose(jvp()))/dot_general | solution.py:9
  457.5 659.1 %collective-permute-start.28 = (f32[1,320,640]{2,1,0:T(8,128)}, f32[1,320,640]{2,1,0:T(8,128)}, u32[]{:S(2)}, u32[]{:S(2)}) collective-permute-start(f32[1,320,640]{2,1,0:T(8,128)} %get-tuple-element.45), channel_id=42, source_target_pairs={{0,1},{1,2},{2,3},{3,4},{4,5},{5,6},{6,7},{7,0},{8,9},{9,10},{10,1... | collective-permute-start | bytes 2457608 | tf_op jit(solution)/vmap(transpose(jvp()))/dot_general | solution.py:9
  523.9 21.5 %collective-permute-start.20 = (f32[1,320,640]{2,1,0:T(8,128)}, f32[1,320,640]{2,1,0:T(8,128)S(1)}, u32[]{:S(2)}, u32[]{:S(2)}) collective-permute-start(f32[1,320,640]{2,1,0:T(8,128)} %broadcast_select_fusion.34), channel_id=45, source_target_pairs={{0,1},{1,2},{2,3},{3,4},{4,5},{5,6},{6,7},{7,0},{8,9},{9,10},{10,1... | collective-permute-start | bytes 2457608 | tf_op jit(solution)/vmap(transpose(jvp()))/dot_general | solution.py:9
  525.2 20.3 %collective-permute-start.21 = (f32[1,320,640]{2,1,0:T(8,128)}, f32[1,320,640]{2,1,0:T(8,128)S(1)}, u32[]{:S(2)}, u32[]{:S(2)}) collective-permute-start(f32[1,320,640]{2,1,0:T(8,128)} %broadcast_select_fusion.35), channel_id=44, source_target_pairs={{0,7},{1,0},{2,1},{3,2},{4,3},{5,4},{6,5},{7,6},{8,15},{9,8},{10,9... | collective-permute-start | bytes 2457608 | tf_op jit(solution)/vmap(transpose(jvp()))/dot_general | solution.py:9
  545.6 21.5 %collective-permute-start.22 = (f32[1,320,640]{2,1,0:T(8,128)S(1)}, f32[1,320,640]{2,1,0:T(8,128)S(1)}, u32[]{:S(2)}, u32[]{:S(2)}) collective-permute-start(f32[1,320,640]{2,1,0:T(8,128)S(1)} %get-tuple-element.506), channel_id=47, source_target_pairs={{0,1},{1,2},{2,3},{3,4},{4,5},{5,6},{6,7},{7,0},{8,9},{9,10},{10,1... | collective-permute-start | bytes 2457608 | tf_op jit(solution)/vmap(transpose(jvp()))/dot_general | solution.py:9
  546.5 20.6 %collective-permute-start.23 = (f32[1,320,640]{2,1,0:T(8,128)S(1)}, f32[1,320,640]{2,1,0:T(8,128)S(1)}, u32[]{:S(2)}, u32[]{:S(2)}) collective-permute-start(f32[1,320,640]{2,1,0:T(8,128)S(1)} %get-tuple-element.507), channel_id=46, source_target_pairs={{0,7},{1,0},{2,1},{3,2},{4,3},{5,4},{6,5},{7,6},{8,15},{9,8},{10,9... | collective-permute-start | bytes 2457608 | tf_op jit(solution)/vmap(transpose(jvp()))/dot_general | solution.py:9
  570.3 21.5 %collective-permute-start.20 = (f32[1,320,640]{2,1,0:T(8,128)}, f32[1,320,640]{2,1,0:T(8,128)S(1)}, u32[]{:S(2)}, u32[]{:S(2)}) collective-permute-start(f32[1,320,640]{2,1,0:T(8,128)} %broadcast_select_fusion.34), channel_id=45, source_target_pairs={{0,1},{1,2},{2,3},{3,4},{4,5},{5,6},{6,7},{7,0},{8,9},{9,10},{10,1... | collective-permute-start | bytes 2457608 | tf_op jit(solution)/vmap(transpose(jvp()))/dot_general | solution.py:9
  571.4 20.4 %collective-permute-start.21 = (f32[1,320,640]{2,1,0:T(8,128)}, f32[1,320,640]{2,1,0:T(8,128)S(1)}, u32[]{:S(2)}, u32[]{:S(2)}) collective-permute-start(f32[1,320,640]{2,1,0:T(8,128)} %broadcast_select_fusion.35), channel_id=44, source_target_pairs={{0,7},{1,0},{2,1},{3,2},{4,3},{5,4},{6,5},{7,6},{8,15},{9,8},{10,9... | collective-permute-start | bytes 2457608 | tf_op jit(solution)/vmap(transpose(jvp()))/dot_general | solution.py:9
  612.9 505.2 %collective-permute-start.29 = (f32[1,320,640]{2,1,0:T(8,128)}, f32[1,320,640]{2,1,0:T(8,128)}, u32[]{:S(2)}, u32[]{:S(2)}) collective-permute-start(f32[1,320,640]{2,1,0:T(8,128)} %get-tuple-element.47), channel_id=48, source_target_pairs={{0,1},{1,2},{2,3},{3,4},{4,5},{5,6},{6,7},{7,0},{8,9},{9,10},{10,1... | collective-permute-start | bytes 2457608 | tf_op jit(solution)/vmap(transpose(jvp()))/dot_general | solution.py:9
  614.9 29.1 %collective-permute-start.8 = (f32[1,80,2560]{2,1,0:T(8,128)}, f32[1,80,2560]{2,1,0:T(8,128)S(1)}, u32[]{:S(2)}, u32[]{:S(2)}) collective-permute-start(f32[1,80,2560]{2,1,0:T(8,128)} %broadcast_select_fusion.28), channel_id=27, source_target_pairs={{0,1},{1,2},{2,3},{3,4},{4,5},{5,6},{6,7},{7,0},{8,9},{9,10},{10,1... | collective-permute-start | bytes 2457608 | tf_op jit(solution)/vmap(transpose(jvp()))/dot_general | solution.py:21
  616.8 27.3 %collective-permute-start.9 = (f32[1,80,2560]{2,1,0:T(8,128)}, f32[1,80,2560]{2,1,0:T(8,128)S(1)}, u32[]{:S(2)}, u32[]{:S(2)}) collective-permute-start(f32[1,80,2560]{2,1,0:T(8,128)} %broadcast_select_fusion.29), channel_id=26, source_target_pairs={{0,7},{1,0},{2,1},{3,2},{4,3},{5,4},{6,5},{7,6},{8,15},{9,8},{10,9... | collective-permute-start | bytes 2457608 | tf_op jit(solution)/vmap(transpose(jvp()))/dot_general | solution.py:21
  668.2 21.6 %collective-permute-start.8 = (f32[1,80,2560]{2,1,0:T(8,128)}, f32[1,80,2560]{2,1,0:T(8,128)S(1)}, u32[]{:S(2)}, u32[]{:S(2)}) collective-permute-start(f32[1,80,2560]{2,1,0:T(8,128)} %broadcast_select_fusion.28), channel_id=27, source_target_pairs={{0,1},{1,2},{2,3},{3,4},{4,5},{5,6},{6,7},{7,0},{8,9},{9,10},{10,1... | collective-permute-start | bytes 2457608 | tf_op jit(solution)/vmap(transpose(jvp()))/dot_general | solution.py:21
  690.8 21.3 %collective-permute-start.10 = (f32[1,80,2560]{2,1,0:T(8,128)}, f32[1,80,2560]{2,1,0:T(8,128)S(1)}, u32[]{:S(2)}, u32[]{:S(2)}) collective-permute-start(f32[1,80,2560]{2,1,0:T(8,128)} %get-tuple-element.479), channel_id=29, source_target_pairs={{0,1},{1,2},{2,3},{3,4},{4,5},{5,6},{6,7},{7,0},{8,9},{9,10},{10,1... | collective-permute-start | bytes 2457608 | tf_op jit(solution)/vmap(transpose(jvp()))/dot_general | solution.py:21
  691.6 20.6 %collective-permute-start.11 = (f32[1,80,2560]{2,1,0:T(8,128)S(1)}, f32[1,80,2560]{2,1,0:T(8,128)}, u32[]{:S(2)}, u32[]{:S(2)}) collective-permute-start(f32[1,80,2560]{2,1,0:T(8,128)S(1)} %get-tuple-element.480), channel_id=28, source_target_pairs={{0,7},{1,0},{2,1},{3,2},{4,3},{5,4},{6,5},{7,6},{8,15},{9,8},{10,9... | collective-permute-start | bytes 2457608 | tf_op jit(solution)/vmap(transpose(jvp()))/dot_general | solution.py:21
  714.4 399.4 %collective-permute-start.26 = (f32[1,80,2560]{2,1,0:T(8,128)}, f32[1,80,2560]{2,1,0:T(8,128)}, u32[]{:S(2)}, u32[]{:S(2)}) collective-permute-start(f32[1,80,2560]{2,1,0:T(8,128)} %get-tuple-element.41), channel_id=30, source_target_pairs={{0,1},{1,2},{2,3},{3,4},{4,5},{5,6},{6,7},{7,0},{8,9},{9,10},{10,1... | collective-permute-start | bytes 2457608 | tf_op jit(solution)/vmap(transpose(jvp()))/dot_general | solution.py:21
  812.7 20.9 %collective-permute-start.12 = (f32[1,80,2560]{2,1,0:T(8,128)}, f32[1,80,2560]{2,1,0:T(8,128)S(1)}, u32[]{:S(2)}, u32[]{:S(2)}) collective-permute-start(f32[1,80,2560]{2,1,0:T(8,128)} %broadcast_select_fusion.30), channel_id=33, source_target_pairs={{0,1},{1,2},{2,3},{3,4},{4,5},{5,6},{6,7},{7,0},{8,9},{9,10},{10,1... | collective-permute-start | bytes 2457608 | tf_op jit(solution)/vmap(transpose(jvp()))/dot_general | solution.py:21
  835.0 22.0 %collective-permute-start.14 = (f32[1,80,2560]{2,1,0:T(8,128)}, f32[1,80,2560]{2,1,0:T(8,128)S(1)}, u32[]{:S(2)}, u32[]{:S(2)}) collective-permute-start(f32[1,80,2560]{2,1,0:T(8,128)} %get-tuple-element.488), channel_id=35, source_target_pairs={{0,1},{1,2},{2,3},{3,4},{4,5},{5,6},{6,7},{7,0},{8,9},{9,10},{10,1... | collective-permute-start | bytes 2457608 | tf_op jit(solution)/vmap(transpose(jvp()))/dot_general | solution.py:21
  835.3 21.6 %collective-permute-start.15 = (f32[1,80,2560]{2,1,0:T(8,128)}, f32[1,80,2560]{2,1,0:T(8,128)}, u32[]{:S(2)}, u32[]{:S(2)}) collective-permute-start(f32[1,80,2560]{2,1,0:T(8,128)} %get-tuple-element.489), channel_id=34, source_target_pairs={{0,7},{1,0},{2,1},{3,2},{4,3},{5,4},{6,5},{7,6},{8,15},{9,8},{10,9... | collective-permute-start | bytes 2457608 | tf_op jit(solution)/vmap(transpose(jvp()))/dot_general | solution.py:21
  861.3 21.1 %collective-permute-start.12 = (f32[1,80,2560]{2,1,0:T(8,128)}, f32[1,80,2560]{2,1,0:T(8,128)S(1)}, u32[]{:S(2)}, u32[]{:S(2)}) collective-permute-start(f32[1,80,2560]{2,1,0:T(8,128)} %broadcast_select_fusion.30), channel_id=33, source_target_pairs={{0,1},{1,2},{2,3},{3,4},{4,5},{5,6},{6,7},{7,0},{8,9},{9,10},{10,1... | collective-permute-start | bytes 2457608 | tf_op jit(solution)/vmap(transpose(jvp()))/dot_general | solution.py:21
  862.2 20.2 %collective-permute-start.13 = (f32[1,80,2560]{2,1,0:T(8,128)}, f32[1,80,2560]{2,1,0:T(8,128)S(1)}, u32[]{:S(2)}, u32[]{:S(2)}) collective-permute-start(f32[1,80,2560]{2,1,0:T(8,128)} %broadcast_select_fusion.31), channel_id=32, source_target_pairs={{0,7},{1,0},{2,1},{3,2},{4,3},{5,4},{6,5},{7,6},{8,15},{9,8},{10,9... | collective-permute-start | bytes 2457608 | tf_op jit(solution)/vmap(transpose(jvp()))/dot_general | solution.py:21
  883.7 19.9 %collective-permute-start.14 = (f32[1,80,2560]{2,1,0:T(8,128)}, f32[1,80,2560]{2,1,0:T(8,128)S(1)}, u32[]{:S(2)}, u32[]{:S(2)}) collective-permute-start(f32[1,80,2560]{2,1,0:T(8,128)} %get-tuple-element.488), channel_id=35, source_target_pairs={{0,1},{1,2},{2,3},{3,4},{4,5},{5,6},{6,7},{7,0},{8,9},{9,10},{10,1... | collective-permute-start | bytes 2457608 | tf_op jit(solution)/vmap(transpose(jvp()))/dot_general | solution.py:21
  883.7 19.9 %collective-permute-start.15 = (f32[1,80,2560]{2,1,0:T(8,128)}, f32[1,80,2560]{2,1,0:T(8,128)}, u32[]{:S(2)}, u32[]{:S(2)}) collective-permute-start(f32[1,80,2560]{2,1,0:T(8,128)} %get-tuple-element.489), channel_id=34, source_target_pairs={{0,7},{1,0},{2,1},{3,2},{4,3},{5,4},{6,5},{7,6},{8,15},{9,8},{10,9... | collective-permute-start | bytes 2457608 | tf_op jit(solution)/vmap(transpose(jvp()))/dot_general | solution.py:21
  908.0 21.9 %collective-permute-start = (f32[1,80,2560]{2,1,0:T(8,128)}, f32[1,80,2560]{2,1,0:T(8,128)S(1)}, u32[]{:S(2)}, u32[]{:S(2)}) collective-permute-start(f32[1,80,2560]{2,1,0:T(8,128)} %broadcast_select_fusion.24), channel_id=15, source_target_pairs={{0,1},{1,2},{2,3},{3,4},{4,5},{5,6},{6,7},{7,0},{8,9},{9,10},{10,1... | collective-permute-start | bytes 2457608 | tf_op jit(solution)/vmap(transpose(jvp()))/dot_general | solution.py:20
  908.9 20.9 %collective-permute-start.1 = (f32[1,80,2560]{2,1,0:T(8,128)}, f32[1,80,2560]{2,1,0:T(8,128)S(1)}, u32[]{:S(2)}, u32[]{:S(2)}) collective-permute-start(f32[1,80,2560]{2,1,0:T(8,128)} %broadcast_select_fusion.25), channel_id=14, source_target_pairs={{0,7},{1,0},{2,1},{3,2},{4,3},{5,4},{6,5},{7,6},{8,15},{9,8},{10,9... | collective-permute-start | bytes 2457608 | tf_op jit(solution)/vmap(transpose(jvp()))/dot_general | solution.py:20
  931.2 20.4 %collective-permute-start.2 = (f32[1,80,2560]{2,1,0:T(8,128)}, f32[1,80,2560]{2,1,0:T(8,128)S(1)}, u32[]{:S(2)}, u32[]{:S(2)}) collective-permute-start(f32[1,80,2560]{2,1,0:T(8,128)} %get-tuple-element.461), channel_id=17, source_target_pairs={{0,1},{1,2},{2,3},{3,4},{4,5},{5,6},{6,7},{7,0},{8,9},{9,10},{10,1... | collective-permute-start | bytes 2457608 | tf_op jit(solution)/vmap(transpose(jvp()))/dot_general | solution.py:20
  931.2 20.4 %collective-permute-start.3 = (f32[1,80,2560]{2,1,0:T(8,128)}, f32[1,80,2560]{2,1,0:T(8,128)}, u32[]{:S(2)}, u32[]{:S(2)}) collective-permute-start(f32[1,80,2560]{2,1,0:T(8,128)} %get-tuple-element.462), channel_id=16, source_target_pairs={{0,7},{1,0},{2,1},{3,2},{4,3},{5,4},{6,5},{7,6},{8,15},{9,8},{10,9... | collective-permute-start | bytes 2457608 | tf_op jit(solution)/vmap(transpose(jvp()))/dot_general | solution.py:20
  955.9 21.4 %collective-permute-start = (f32[1,80,2560]{2,1,0:T(8,128)}, f32[1,80,2560]{2,1,0:T(8,128)S(1)}, u32[]{:S(2)}, u32[]{:S(2)}) collective-permute-start(f32[1,80,2560]{2,1,0:T(8,128)} %broadcast_select_fusion.24), channel_id=15, source_target_pairs={{0,1},{1,2},{2,3},{3,4},{4,5},{5,6},{6,7},{7,0},{8,9},{9,10},{10,1... | collective-permute-start | bytes 2457608 | tf_op jit(solution)/vmap(transpose(jvp()))/dot_general | solution.py:20
  956.9 20.4 %collective-permute-start.1 = (f32[1,80,2560]{2,1,0:T(8,128)}, f32[1,80,2560]{2,1,0:T(8,128)S(1)}, u32[]{:S(2)}, u32[]{:S(2)}) collective-permute-start(f32[1,80,2560]{2,1,0:T(8,128)} %broadcast_select_fusion.25), channel_id=14, source_target_pairs={{0,7},{1,0},{2,1},{3,2},{4,3},{5,4},{6,5},{7,6},{8,15},{9,8},{10,9... | collective-permute-start | bytes 2457608 | tf_op jit(solution)/vmap(transpose(jvp()))/dot_general | solution.py:20
  978.6 19.9 %collective-permute-start.2 = (f32[1,80,2560]{2,1,0:T(8,128)}, f32[1,80,2560]{2,1,0:T(8,128)S(1)}, u32[]{:S(2)}, u32[]{:S(2)}) collective-permute-start(f32[1,80,2560]{2,1,0:T(8,128)} %get-tuple-element.461), channel_id=17, source_target_pairs={{0,1},{1,2},{2,3},{3,4},{4,5},{5,6},{6,7},{7,0},{8,9},{9,10},{10,1... | collective-permute-start | bytes 2457608 | tf_op jit(solution)/vmap(transpose(jvp()))/dot_general | solution.py:20
  978.6 19.9 %collective-permute-start.3 = (f32[1,80,2560]{2,1,0:T(8,128)}, f32[1,80,2560]{2,1,0:T(8,128)}, u32[]{:S(2)}, u32[]{:S(2)}) collective-permute-start(f32[1,80,2560]{2,1,0:T(8,128)} %get-tuple-element.462), channel_id=16, source_target_pairs={{0,7},{1,0},{2,1},{3,2},{4,3},{5,4},{6,5},{7,6},{8,15},{9,8},{10,9... | collective-permute-start | bytes 2457608 | tf_op jit(solution)/vmap(transpose(jvp()))/dot_general | solution.py:20
  1001.7 21.3 %collective-permute-start.4 = (f32[1,80,2560]{2,1,0:T(8,128)}, f32[1,80,2560]{2,1,0:T(8,128)S(1)}, u32[]{:S(2)}, u32[]{:S(2)}) collective-permute-start(f32[1,80,2560]{2,1,0:T(8,128)} %broadcast_select_fusion.26), channel_id=21, source_target_pairs={{0,1},{1,2},{2,3},{3,4},{4,5},{5,6},{6,7},{7,0},{8,9},{9,10},{10,1... | collective-permute-start | bytes 2457608 | tf_op jit(solution)/vmap(transpose(jvp()))/dot_general | solution.py:20
  1002.7 20.3 %collective-permute-start.5 = (f32[1,80,2560]{2,1,0:T(8,128)}, f32[1,80,2560]{2,1,0:T(8,128)S(1)}, u32[]{:S(2)}, u32[]{:S(2)}) collective-permute-start(f32[1,80,2560]{2,1,0:T(8,128)} %broadcast_select_fusion.27), channel_id=20, source_target_pairs={{0,7},{1,0},{2,1},{3,2},{4,3},{5,4},{6,5},{7,6},{8,15},{9,8},{10,9... | collective-permute-start | bytes 2457608 | tf_op jit(solution)/vmap(transpose(jvp()))/dot_general | solution.py:20
  1048.5 21.5 %collective-permute-start.4 = (f32[1,80,2560]{2,1,0:T(8,128)}, f32[1,80,2560]{2,1,0:T(8,128)S(1)}, u32[]{:S(2)}, u32[]{:S(2)}) collective-permute-start(f32[1,80,2560]{2,1,0:T(8,128)} %broadcast_select_fusion.26), channel_id=21, source_target_pairs={{0,1},{1,2},{2,3},{3,4},{4,5},{5,6},{6,7},{7,0},{8,9},{9,10},{10,1... | collective-permute-start | bytes 2457608 | tf_op jit(solution)/vmap(transpose(jvp()))/dot_general | solution.py:20
  1049.5 20.5 %collective-permute-start.5 = (f32[1,80,2560]{2,1,0:T(8,128)}, f32[1,80,2560]{2,1,0:T(8,128)S(1)}, u32[]{:S(2)}, u32[]{:S(2)}) collective-permute-start(f32[1,80,2560]{2,1,0:T(8,128)} %broadcast_select_fusion.27), channel_id=20, source_target_pairs={{0,7},{1,0},{2,1},{3,2},{4,3},{5,4},{6,5},{7,6},{8,15},{9,8},{10,9... | collective-permute-start | bytes 2457608 | tf_op jit(solution)/vmap(transpose(jvp()))/dot_general | solution.py:20
  1071.4 20.0 %collective-permute-start.6 = (f32[1,80,2560]{2,1,0:T(8,128)}, f32[1,80,2560]{2,1,0:T(8,128)S(1)}, u32[]{:S(2)}, u32[]{:S(2)}) collective-permute-start(f32[1,80,2560]{2,1,0:T(8,128)} %get-tuple-element.470), channel_id=23, source_target_pairs={{0,1},{1,2},{2,3},{3,4},{4,5},{5,6},{6,7},{7,0},{8,9},{9,10},{10,1... | collective-permute-start | bytes 2457608 | tf_op jit(solution)/vmap(transpose(jvp()))/dot_general | solution.py:20
  1071.4 20.0 %collective-permute-start.7 = (f32[1,80,2560]{2,1,0:T(8,128)}, f32[1,80,2560]{2,1,0:T(8,128)}, u32[]{:S(2)}, u32[]{:S(2)}) collective-permute-start(f32[1,80,2560]{2,1,0:T(8,128)} %get-tuple-element.471), channel_id=22, source_target_pairs={{0,7},{1,0},{2,1},{3,2},{4,3},{5,4},{6,5},{7,6},{8,15},{9,8},{10,9... | collective-permute-start | bytes 2457608 | tf_op jit(solution)/vmap(transpose(jvp()))/dot_general | solution.py:20
  1093.6 21.7 %collective-permute-start.27 = (f32[1,80,2560]{2,1,0:T(8,128)}, f32[1,80,2560]{2,1,0:T(8,128)}, u32[]{:S(2)}, u32[]{:S(2)}) collective-permute-start(f32[1,80,2560]{2,1,0:T(8,128)} %get-tuple-element.43), channel_id=36, source_target_pairs={{0,1},{1,2},{2,3},{3,4},{4,5},{5,6},{6,7},{7,0},{8,9},{9,10},{10,1... | collective-permute-start | bytes 2457608 | tf_op jit(solution)/vmap(transpose(jvp()))/dot_general | solution.py:21
  1113.7 22.3 %collective-permute-start.25 = (f32[1,80,2560]{2,1,0:T(8,128)}, f32[1,80,2560]{2,1,0:T(8,128)S(1)}, u32[]{:S(2)}, u32[]{:S(2)}) collective-permute-start(f32[1,80,2560]{2,1,0:T(8,128)} %get-tuple-element.39), channel_id=24, source_target_pairs={{0,1},{1,2},{2,3},{3,4},{4,5},{5,6},{6,7},{7,0},{8,9},{9,10},{10,1... | collective-permute-start | bytes 2457608 | tf_op jit(solution)/vmap(transpose(jvp()))/dot_general | solution.py:20
  (78 other events, 1976.1 us)
Sparse Core Ops, SparseCore 0:
  9.6 41.6 all-gather.29
  53.0 38.0 all-gather.31
  92.7 38.0 all-gather.33
  132.3 38.0 all-gather.37
  172.0 38.0 all-gather.39
  211.6 38.0 all-gather.35
where the time goes:
time: 1160 us; the launch traced here: 1140 us
  matrix products  513 us (44%)
  waiting for transfers between devices  258 us (22%)
  other arithmetic  133 us (11%)
  local copies, waits for them, and re-layouts  111 us (10%)
  starting transfers between devices  88.6 us (8%)
  loops' own time  25.4 us (2%)
  between operations  14.9 us (1%)
    dot_general x12, matrix products, layer(): gate = jnp.dot(a, w['w_gate'], preferred_element_type=jnp.float32)  191 us
    dot_general x12, matrix products, layer(): up = jnp.dot(a, w['w_up'], preferred_element_type=jnp.float32)  163 us
    dot_general x11, matrix products, matmul(): jnp.dot(a, w, preferred_element_type=jnp.float32).astype(jnp.bfloat16)  158 us
    unnamed x59, local copies, waits for them, and re-layouts  96.1 us
    dot_general x18, waiting for transfers between devices, layer(): gate = jnp.dot(a, w['w_gate'], preferred_element_type=jnp.float32)  80.1 us
    dot_general x18, waiting for transfers between devices, layer(): up = jnp.dot(a, w['w_up'], preferred_element_type=jnp.float32)  74.2 us
    dot_general x18, waiting for transfers between devices, matmul(): jnp.dot(a, w, preferred_element_type=jnp.float32).astype(jnp.bfloat16)  63.4 us
    squeeze x6, waiting for transfers between devices, stack(): h = layer(h, {name: w[number] for name, w in weights.items()})  38.9 us
  transfers between devices with their start and end apart: 60, of which 30 were waited for; matrix products, arithmetic and copies ran while one was open for 55% of the time, Pallas kernels for 0%

commit v1 on v0

v1 whole, which is shorter than its diff:
```python
import functools

import jax
import jax.numpy as jnp
from jax import lax
from jax.experimental import pallas as pl
from jax.experimental.pallas import tpu as pltpu
from jax.sharding import Mesh, PartitionSpec as P

GROUPS = ((0, 1), (2, 3, 4))
EXCHANGES = (0, 2, 4, 6)
NB = 5
TF = 512
TB = 512
SUB = 256
VMEM = 67_000_000
F32 = jnp.float32
BF16 = jnp.bfloat16
Z, C = 4, 2


def mm(a, b):
    return jnp.dot(a, b, preferred_element_type=F32)


def mm_nt(a, b):
    return lax.dot_general(a, b, (((1,), (1,)), ((), ())), preferred_element_type=F32)


def mm_tn(a, b):
    return lax.dot_general(a, b, (((0,), (0,)), ((), ())), preferred_element_type=F32)


def scale_of(wide):
    return lax.rsqrt(jnp.mean(wide * wide, -1, keepdims=True) + 1e-6)


def unpack(core_ref, mine_ref, other_ref, wg, wu, wd):
    dr = wg.shape[0] // (Z * C)
    fr = wd.shape[0] // (Z * C)
    for w_ref, c in ((mine_ref, core_ref[0]), (other_ref, 1 - core_ref[0])):
        for z in range(Z):
            rows = pl.ds(pl.multiple_of(z * C * dr + c * dr, 16), dr)
            for k in range(wg.shape[1] // 128):
                wg[rows, 128 * k : 128 * k + 128] = w_ref[z, 0, dr * k : dr * k + dr, :]
                wu[rows, 128 * k : 128 * k + 128] = w_ref[z, 1, dr * k : dr * k + dr, :]
            rows = pl.ds(pl.multiple_of(c * Z * fr + z * fr, 16), fr)
            for k in range(wd.shape[1] // 128):
                wd[rows, 128 * k : 128 * k + 128] = w_ref[z, 2, fr * k : fr * k + fr, :]


def forward_kernel(first, last, *refs):
    refs = list(refs)
    h_ref = refs.pop(0) if first or last else None
    a_ref = None if first else refs.pop(0)
    w_refs = [refs.pop(0) for _ in range(3)]
    acc_ref = None if first else refs.pop(0)
    gate_ref, up_ref = refs.pop(0), refs.pop(0)
    if first:
        a_out, acc_out = refs.pop(0), refs.pop(0)
    elif last:
        h_out, a_out = refs.pop(0), refs.pop(0)
    else:
        acc_out = refs.pop(0)
    wg, wu, wd = refs

    @pl.when(pl.program_id(0) == 0)
    def _():
        unpack(*w_refs, wg, wu, wd)

    for s in range(TF // SUB):
        rows = slice(s * SUB, s * SUB + SUB)
        if first:
            wide = h_ref[rows].astype(F32)
            a = (wide * scale_of(wide)).astype(BF16)
            a_out[rows] = a
        else:
            a = a_ref[rows]
        gate = mm(a, wg[...])
        up = mm(a, wu[...])
        gate_ref[rows] = gate
        up_ref[rows] = up
        sig = 0.5 * jnp.tanh(0.5 * gate) + 0.5
        p = (gate * sig * up).astype(BF16)
        o = mm(p, wd[...])
        if not first:
            o = o + acc_ref[rows]
        if last:
            h = h_ref[rows] + o.astype(BF16)
            h_out[rows] = h
            wide = h.astype(F32)
            a_out[rows] = (wide * scale_of(wide)).astype(BF16)
        else:
            acc_out[rows] = o


def backward_kernel(first, last, saved, *refs):
    refs = list(refs)
    a_ref, dy_ref = refs.pop(0), refs.pop(0)
    w_refs = [refs.pop(0) for _ in range(3)]
    if saved:
        gate_ref, up_ref = refs.pop(0), refs.pop(0)
    acc_ref = None if first else refs.pop(0)
    h_ref = refs.pop(0) if last else None
    dw_out, out = refs.pop(0), refs.pop(0)
    wg, wu, wd, dwg, dwu, dwd, p_s, dg_s, du_s = refs
    step = pl.program_id(0)

    @pl.when(step == 0)
    def _():
        unpack(*w_refs, wg, wu, wd)
        dwg[...] = jnp.zeros_like(dwg)
        dwu[...] = jnp.zeros_like(dwu)
        dwd[...] = jnp.zeros_like(dwd)

    for s in range(TB // SUB):
        rows = slice(s * SUB, s * SUB + SUB)
        dp = mm_nt(dy_ref[rows], wd[...]).astype(BF16).astype(F32)
        if saved:
            gate, up = gate_ref[rows], up_ref[rows]
        else:
            gate, up = mm(a_ref[rows], wg[...]), mm(a_ref[rows], wu[...])
        sig = 0.5 * jnp.tanh(0.5 * gate) + 0.5
        silu = gate * sig
        p_s[rows] = (silu * up).astype(BF16)
        du_s[rows] = (dp * silu).astype(BF16)
        dg_s[rows] = (dp * up * (sig + silu * (1.0 - sig))).astype(BF16)
        da = mm_nt(dg_s[rows], wg[...]) + mm_nt(du_s[rows], wu[...])
        if not first:
            da = da + acc_ref[rows]
        if last:
            da = da.astype(BF16).astype(F32)
            wide = h_ref[rows].astype(F32)
            r = scale_of(wide)
            inner = jnp.mean(da * wide, -1, keepdims=True)
            dh = da * r - wide * (r * r * r * inner)
            out[rows] = dy_ref[rows] + dh.astype(BF16)
        else:
            out[rows] = da
    dwg[...] += mm_tn(a_ref[...], dg_s[...])
    dwu[...] += mm_tn(a_ref[...], du_s[...])
    dwd[...] += mm_tn(dy_ref[...], p_s[...])

    @pl.when(step == pl.num_programs(0) - 1)
    def _():
        dr = dwg.shape[0] // (Z * C)
        fr = dwd.shape[1] // (Z * C)
        for k in range(dwg.shape[1] // 128):
            for c in range(C):
                for z in range(Z):
                    r = (z * C + c) * dr
                    dw_out[c, z, 0, dr * k : dr * k + dr, :] = dwg[r : r + dr, 128 * k : 128 * k + 128].astype(BF16)
                    dw_out[c, z, 1, dr * k : dr * k + dr, :] = dwu[r : r + dr, 128 * k : 128 * k + 128].astype(BF16)
        for k in range(dwd.shape[0] // 128):
            block = jnp.transpose(dwd[128 * k : 128 * k + 128, :]).astype(BF16)
            for c in range(C):
                for z in range(Z):
                    r = (c * Z + z) * fr
                    dw_out[c, z, 2, fr * k : fr * k + fr, :] = block[r : r + fr, :]


def rows_spec(t, width):
    return pl.BlockSpec((t, width), lambda i: (i, 0))


def whole_spec(shape):
    return pl.BlockSpec(shape, lambda i: (0,) * len(shape))


def params():
    return pltpu.CompilerParams(dimension_semantics=("arbitrary",), vmem_limit_bytes=VMEM)


def weights_scratch(d, fb):
    return [pltpu.VMEM((d, fb), BF16), pltpu.VMEM((d, fb), BF16), pltpu.VMEM((fb, d), BF16)]


def weights_args(w):
    core, mine, other, n = w
    spec = pl.BlockSpec((Z, None, *mine.shape[2:]), lambda i: (0, n, 0, 0, 0))
    return [core, mine, other], [pl.BlockSpec(memory_space=pltpu.SMEM), spec, spec]


def forward(first, last, h, a, w, acc, fb):
    n, d = h.shape
    full = jax.ShapeDtypeStruct
    args, specs = [], []
    if first or last:
        args.append(h)
        specs.append(rows_spec(TF, d))
    if not first:
        args.append(a)
        specs.append(rows_spec(TF, d))
    w_args, w_specs = weights_args(w)
    args += w_args
    specs += w_specs
    alias = {}
    outs = [(full((n, fb), F32), rows_spec(TF, fb))] * 2
    if first:
        outs += [(full((n, d), BF16), rows_spec(TF, d)), (full((n, d), F32), rows_spec(TF, d))]
    elif last:
        outs += [(full((n, d), BF16), rows_spec(TF, d))] * 2
    else:
        outs += [(full((n, d), F32), rows_spec(TF, d))]
    if not first:
        if not last:
            alias = {len(args): 2}
        args.append(acc)
        specs.append(rows_spec(TF, d))
    return pl.pallas_call(
        functools.partial(forward_kernel, first, last),
        grid=(n // TF,),
        out_shape=[o for o, _ in outs],
        in_specs=specs,
        out_specs=[s for _, s in outs],
        scratch_shapes=weights_scratch(d, fb),
        input_output_aliases=alias,
        compiler_params=params(),
        cost_estimate=pl.CostEstimate(flops=6 * n * d * fb, bytes_accessed=n * (16 * d + 8 * fb), transcendentals=n * fb),
        name="mlp_fwd",
    )(*args)


def backward(first, last, saved, a, dy, w, gates, acc, h, fb):
    n, d = a.shape
    w_args, w_specs = weights_args(w)
    grad = (C, Z, *w_args[1].shape[2:])
    full = jax.ShapeDtypeStruct
    args, specs = [a, dy, *w_args], [rows_spec(TB, d), rows_spec(TB, d), *w_specs]
    if saved:
        args += list(gates)
        specs += [rows_spec(TB, fb)] * 2
    alias = {}
    if not first:
        if not last:
            alias = {len(args): 1}
        args.append(acc)
        specs.append(rows_spec(TB, d))
    if last:
        args.append(h)
        specs.append(rows_spec(TB, d))
    return pl.pallas_call(
        functools.partial(backward_kernel, first, last, saved),
        grid=(n // TB,),
        out_shape=[full(grad, BF16), full((n, d), BF16 if last else F32)],
        in_specs=specs,
        out_specs=[whole_spec(grad), rows_spec(TB, d)],
        scratch_shapes=weights_scratch(d, fb) + [pltpu.VMEM((d, fb), F32)] * 3 + [pltpu.VMEM((TB, fb), BF16)] * 3,
        input_output_aliases=alias,
        compiler_params=params(),
        cost_estimate=pl.CostEstimate(
            flops=(12 if saved else 16) * n * d * fb, bytes_accessed=n * (12 * d + (8 * fb if saved else 0)), transcendentals=n * fb
        ),
        name="mlp_bwd",
    )(*args)


def pack_kernel(layers, groups, wg_ref, wu_ref, wd_ref, *outs):
    dr = wg_ref.shape[1]
    fr = wd_ref.shape[1] // NB
    span = NB * fr
    for l in range(layers):
        for g, group in enumerate(groups):
            out = outs[l * len(groups) + g]
            for n, j in enumerate(group):
                for m, ref in enumerate((wg_ref, wu_ref)):
                    for k in range(Z * C * fr // 128):
                        c, z = divmod(2 * k, Z)
                        pieces = []
                        for zz in (z, z + 1):
                            start = (zz * C + c) * span + fr * j
                            pieces.append(ref[l, :, start : start + fr])
                        out[n, m, dr * k : dr * k + dr, :] = jnp.concatenate(pieces, 1)
                for k in range(wd_ref.shape[2] // 128):
                    out[n, 2, fr * k : fr * k + fr, :] = wd_ref[l, fr * j : fr * j + fr, 128 * k : 128 * k + 128]


def pack(wg, wu, wd, groups):
    layers = wg.shape[0]
    rows = wg.shape[1] * wg.shape[2] // NB // 128
    shapes = [jax.ShapeDtypeStruct((len(group), 3, rows, 128), BF16) for _ in range(layers) for group in groups]
    outs = pl.pallas_call(
        functools.partial(pack_kernel, layers, groups),
        out_shape=shapes,
        compiler_params=pltpu.CompilerParams(vmem_limit_bytes=VMEM),
        name="pack",
    )(wg, wu, wd)
    return [outs[l * len(groups) : (l + 1) * len(groups)] for l in range(layers)]


def unpack_grads_kernel(layers, *refs):
    gs, (og, ou, od) = refs[: layers * NB], refs[layers * NB :]
    dr = og.shape[1]
    fr = od.shape[1] // NB
    for l in range(layers):
        for j in range(NB):
            g = gs[l * NB + j]
            for m, out in enumerate((og, ou)):
                for k in range(Z * C * fr // 128):
                    c, z = divmod(2 * k, Z)
                    rows = g[m, dr * k : dr * k + dr, :]
                    for half, zz in enumerate((z, z + 1)):
                        start = (zz * C + c) * NB * fr + fr * j
                        out[l, :, start : start + fr] = rows[:, half * fr : half * fr + fr]
            for k in range(od.shape[2] // 128):
                od[l, fr * j : fr * j + fr, 128 * k : 128 * k + 128] = g[2, fr * k : fr * k + fr, :]


def unpack_grads(grads, dr, ff, d):
    layers = len(grads)
    full = jax.ShapeDtypeStruct
    return pl.pallas_call(
        functools.partial(unpack_grads_kernel, layers),
        out_shape=[full((layers, dr, ff), BF16)] * 2 + [full((layers, ff // Z // C, d), BF16)],
        compiler_params=pltpu.CompilerParams(vmem_limit_bytes=VMEM),
        name="unpack",
    )(*[g for layer in grads for g in layer])


def solution(mesh):
    split = Mesh(mesh.devices.reshape(mesh.devices.shape[0], Z, C), ("rep", "z", "core"))

    def body(x, dy, wg, wu, wd):
        layers, dr, ff = wg.shape
        d = x.shape[-1]
        fb = ff // NB
        x, dy = x[0], dy[0]
        core = lax.axis_index("core").astype(jnp.int32).reshape(1)
        packed = [w for layer in pack(wg, wu, wd, GROUPS) for w in layer]
        mine = [lax.all_gather(w, "z") for w in packed]
        gathered = {}
        runs = 0

        def before_kernel(*values):
            nonlocal runs
            for g, run in enumerate(EXCHANGES):
                if run == runs:
                    if run:
                        mine[g], *values = lax.optimization_barrier((mine[g], *values))
                    other = lax.ppermute(mine[g], "core", [(0, 1), (1, 0)])
                    for n, j in enumerate(GROUPS[g % len(GROUPS)]):
                        gathered[g // len(GROUPS), j] = (core, mine[g], other, n)
            runs += 1
            return values

        hs, as_, gates = [x], [], []
        h = x
        a = acc = None
        for l in range(layers - 1):
            gates.append([])
            for j in range(NB):
                first, last = j == 0 and l == 0, j == NB - 1
                (acc,) = before_kernel(acc)
                gate, up, *rest = forward(first, last, h, a, gathered[l, j], acc, fb)
                gates[l].append((gate, up))
                if first:
                    a, acc = rest
                    as_.append(a)
                elif last:
                    h, a = rest
                    hs.append(h)
                    as_.append(a)
                else:
                    (acc,) = rest

        over_core, over_z = [], []
        by_h = dy
        for l in reversed(range(layers)):
            acc = None
            for j in range(NB):
                saved = l < layers - 1
                k = len(over_core)
                by_h, acc = before_kernel(by_h, acc)
                while len(over_z) <= k - 2:
                    n = len(over_z)
                    done = over_z[n - 1] if n else None
                    by_h, acc, over_core[n], done = lax.optimization_barrier((by_h, acc, over_core[n], done))
                    if n:
                        over_z[n - 1] = done
                    over_z.append(lax.psum_scatter(over_core[n], "z", scatter_dimension=0, tiled=False))
                dw, acc = backward(
                    j == 0, j == NB - 1, saved, as_[l], by_h, gathered[l, j], gates[l][j] if saved else None, acc, hs[l], fb
                )
                over_core.append(lax.psum_scatter(dw, "core", scatter_dimension=0, tiled=False))
            by_h = acc
        for part in over_core[len(over_z) :]:
            over_z.append(lax.psum_scatter(part, "z", scatter_dimension=0, tiled=False))
        grads = [over_z[NB * (layers - 1 - l) :][:NB] for l in range(layers)]
        return (by_h[None], *unpack_grads(grads, dr, ff, d))

    rows, weights, outs = P(("rep", "z", "core")), P(None, ("z", "core")), P("rep", ("z", "core"))
    return jax.shard_map(
        body, mesh=split, in_specs=(rows, rows, weights, weights, weights), out_specs=(rows, outs, outs, outs), check_vma=False
    )
```

time: 1160 us -> 670 us (0.58); the launches traced: 1140 us -> 666 us
  matrix products: 513 us -> 0 us
  Pallas kernels: 0 us -> 416 us
  other arithmetic: 133 us -> 0 us
  local copies, waits for them, and re-layouts: 111 us -> 0 us
  starting transfers between devices: 88.6 us -> 2.67 us
  loops' own time: 25.4 us -> 0 us
  waiting for transfers between devices: 258 us -> 233 us
    dot_general x35 -> x0, matrix products: 513 us -> none  [the longest x12 191 us: layer(): gate = jnp.dot(a, w['w_gate'], preferred_element_type=jnp.float32)]
    pallas_call x0 -> x17, Pallas kernels: none -> 416 us  [the longest x10 306 us: backward(): pl.pallas_call(functools.partial(backward_kernel, first, last, saved), gr...]
    dot_general x54 -> x0, waiting for transfers between devices: 218 us -> none  [the longest x18 80.1 us: layer(): gate = jnp.dot(a, w['w_gate'], preferred_element_type=jnp.float32)]
    reduce_scatter x0 -> x20, waiting for transfers between devices: none -> 148 us  [the longest x8 75.5 us: body(): lax.psum_scatter(over_core[n], 'z', scatter_dimension=0, tiled=False)]
    unnamed x59 -> x0, local copies, waits for them, and re-layouts: 96.1 us -> none
    dot_general x54 -> x0, starting transfers between devices: 88.4 us -> none  [the longest x18 31.2 us: matmul(): jnp.dot(a, w, preferred_element_type=jnp.float32).astype(jnp.bfloat16)]
    all_gather x0 -> x4, waiting for transfers between devices: none -> 66.1 us  [body(): mine = [lax.all_gather(w, 'z') for w in packed]]
    dot_general x56 -> x0, other arithmetic: 59.4 us -> none
  transfers between devices with their start and end apart: 60 -> 28, of which waited for: 30 -> 16; matrix products, arithmetic and copies ran while one was open for 55% -> 0% of each run, Pallas kernels for 0% -> 61%
where the time goes in v1:
time: 670 us; the launch traced here: 666 us
  Pallas kernels  416 us (62%)
  waiting for transfers between devices  233 us (35%)
  between operations  14.8 us (2%)
    pallas_call x10, Pallas kernels, backward(): pl.pallas_call(functools.partial(backward_kernel, first, last, saved), gr...  306 us
    pallas_call x5, Pallas kernels, forward(): pl.pallas_call(functools.partial(forward_kernel, first, last), grid=(n //...  102 us
    reduce_scatter x8, waiting for transfers between devices, body(): lax.psum_scatter(over_core[n], 'z', scatter_dimension=0, tiled=False)  75.5 us
    all_gather x4, waiting for transfers between devices, body(): mine = [lax.all_gather(w, 'z') for w in packed]  66.1 us
    reduce_scatter x2, waiting for transfers between devices, body(): over_z.append(lax.psum_scatter(part, 'z', scatter_dimension=0, tiled=False))  54.5 us
    reduce_scatter x10, waiting for transfers between devices, body(): lax.psum_scatter(dw, 'core', scatter_dimension=0, tiled=False)  18.4 us
    ppermute x4, waiting for transfers between devices, before_kernel(): other = lax.ppermute(mine[g], 'core', [(0, 1), (1, 0)])  13.9 us
  transfers between devices with their start and end apart: 28, of which 16 were waited for; matrix products, arithmetic and copies ran while one was open for 0% of the time, Pallas kernels for 61%

profile of v1, /device:TPU:0, one launch (start us, length us, event | category | flops | bytes accessed | tf_op | source)
XLA Modules:
  0.0 666.0 jit_solution(9829788748372061552)
XLA Ops:
  7.2 3.5 pack.1
  10.8 0.0 all-gather.11.cloned.1.call-start
  10.8 0.7 all-gather.11.cloned.1.call-update
  11.6 45.2 %all-gather.9.cloned.1.call-done = bf16[8,3,320,128]{3,2,1,0:T(8,128)(2,1)} async-done(((bf16[2,3,320,128]{3,2,1,0:T(8,128)(2,1)}), bf16[8,3,320,128]{3,2,1,0:T(8,128)(2,1)}) %all-gather.9.cloned.1.call-update) | async-done | bytes 1966096 | tf_op jit(solution)/shard_map/all_gather | solution.py:330
  56.9 3.8 collective-permute-done.refs_3_.refs_4_
  60.7 17.4 %mlp_fwd.5 = (f32[4096,512]{1,0:T(8,128)}, f32[4096,512]{1,0:T(8,128)}, bf16[4096,640]{1,0:T(8,128)(2,1)}, f32[4096,640]{1,0:T(8,128)}) custom-call(bf16[4096,640]{1,0:T(8,128)(2,1)} %bitcast.53, s32[1]{0:T(128)} %bitcast.1.refs_1_.refs_2_, bf16[4,2,3,320,128]{4,3,2,1,0:T(8,128)(2,1)} %bitcast.68, ...), custom_call_target="tpu_custom_call" | custom-call | flops 8053063680 | bytes 58720256 | tf_op jit(solution)/shard_map/mlp_fwd/pallas_call | solution.py:210
  78.1 20.6 %mlp_fwd.6 = (f32[4096,512]{1,0:T(8,128)}, f32[4096,512]{1,0:T(8,128)}, f32[4096,640]{1,0:T(8,128)}) custom-call(bf16[4096,640]{1,0:T(8,128)(2,1)} %get-tuple-element.86.refs_0_.refs_1_, s32[1]{0:T(128)} %bitcast.1.refs_1_.refs_2_, bf16[4,2,3,320,128]{4,3,2,1,0:T(8,128)(2,1)} %bitcast.69, ...), custom_call_target="tpu_custom_call", output_to_operand_aliasing={{2}: (4, {})} | custom-call | flops 8053063680 | bytes 58720256 | tf_op jit(solution)/shard_map/mlp_fwd/pallas_call | solution.py:210
  98.7 18.8 %all-gather.11.cloned.1.call-done = bf16[12,3,320,128]{3,2,1,0:T(8,128)(2,1)} async-done(((bf16[3,3,320,128]{3,2,1,0:T(8,128)(2,1)}), bf16[12,3,320,128]{3,2,1,0:T(8,128)(2,1)}) %all-gather.11.cloned.1.call-update) | async-done | bytes 2949136 | tf_op jit(solution)/shard_map/all_gather | solution.py:330
  117.6 0.3 reduce-scatter.21.cloned.1.call-start
  117.9 5.0 collective-permute-done.1.refs_3_.refs_4_
  122.9 20.6 %mlp_fwd.7 = (f32[4096,512]{1,0:T(8,128)}, f32[4096,512]{1,0:T(8,128)}, f32[4096,640]{1,0:T(8,128)}) custom-call(bf16[4096,640]{1,0:T(8,128)(2,1)} %get-tuple-element.86.refs_0_.refs_1_, s32[1]{0:T(128)} %bitcast.1.refs_1_.refs_2_, bf16[4,3,3,320,128]{4,3,2,1,0:T(8,128)(2,1)} %bitcast.57, ...), custom_call_target="tpu_custom_call", output_to_operand_aliasing={{2}: (4, {})} | custom-call | flops 8053063680 | bytes 58720256 | tf_op jit(solution)/shard_map/mlp_fwd/pallas_call | solution.py:210
  143.5 20.6 %mlp_fwd.8 = (f32[4096,512]{1,0:T(8,128)}, f32[4096,512]{1,0:T(8,128)}, f32[4096,640]{1,0:T(8,128)}) custom-call(bf16[4096,640]{1,0:T(8,128)(2,1)} %get-tuple-element.86.refs_0_.refs_1_, s32[1]{0:T(128)} %bitcast.1.refs_1_.refs_2_, bf16[4,3,3,320,128]{4,3,2,1,0:T(8,128)(2,1)} %bitcast.58, ...), custom_call_target="tpu_custom_call", output_to_operand_aliasing={{2}: (4, {})} | custom-call | flops 8053063680 | bytes 58720256 | tf_op jit(solution)/shard_map/mlp_fwd/pallas_call | solution.py:210
  164.0 0.2 collective-permute-start.2
  164.2 23.3 %mlp_fwd.9 = (f32[4096,512]{1,0:T(8,128)}, f32[4096,512]{1,0:T(8,128)}, bf16[4096,640]{1,0:T(8,128)(2,1)}, bf16[4096,640]{1,0:T(8,128)(2,1)}) custom-call(bf16[4096,640]{1,0:T(8,128)(2,1)} %bitcast.54, bf16[4096,640]{1,0:T(8,128)(2,1)} %get-tuple-element.86.refs_0_.refs_1_, s32[1]{0:T(128)} %bitcast.1.refs_1_.refs_2_, bf16[4,3,3,320,128]{4,3,2,1,0:T(8,128)(2,1)} %bitcast.59, ...), custom_call_target="tpu_custom_call" | custom-call | flops 8053063680 | bytes 58720256 | tf_op jit(solution)/shard_map/mlp_fwd/pallas_call | solution.py:210
  187.5 32.1 %mlp_bwd.10 = (bf16[2,4,3,320,128]{4,3,2,1,0:T(8,128)(2,1)}, f32[4096,640]{1,0:T(8,128)}) custom-call(bf16[4096,640]{1,0:T(8,128)(2,1)} %get-tuple-element.96.refs_0_, bf16[4096,640]{1,0:T(8,128)(2,1)} %bitcast.48, s32[1]{0:T(128)} %bitcast.1.refs_1_.refs_2_, bf16[4,2,3,320,128]{4,3,2,1,0:T(8,128)(2,1)} %bitcast.73, ...), custom_call_target="tpu_custom_call" | custom-call | flops 21474836480 | bytes 31457280 | tf_op jit(solution)/shard_map/mlp_bwd/pallas_call | solution.py:242
  219.6 0.6 reduce-scatter.23.cloned.1.call-start
  220.2 2.1 all-gather.15.cloned.1.call-done
  222.3 32.9 %mlp_bwd.11 = (bf16[2,4,3,320,128]{4,3,2,1,0:T(8,128)(2,1)}, f32[4096,640]{1,0:T(8,128)}) custom-call(bf16[4096,640]{1,0:T(8,128)(2,1)} %get-tuple-element.96.refs_0_, bf16[4096,640]{1,0:T(8,128)(2,1)} %bitcast.49, s32[1]{0:T(128)} %bitcast.1.refs_1_.refs_2_, bf16[4,2,3,320,128]{4,3,2,1,0:T(8,128)(2,1)} %bitcast.74, ...), custom_call_target="tpu_custom_call", output_to_operand_aliasing={{1}: (5, {})} | custom-call | flops 21474836480 | bytes 31457280 | tf_op jit(solution)/shard_map/mlp_bwd/pallas_call | solution.py:242
  255.3 0.1 collective-permute-start.3
  255.4 0.6 reduce-scatter.25.cloned.1.call-update
  256.1 5.1 collective-permute-done.3.refs_4_
  261.2 32.9 %mlp_bwd.12 = (bf16[2,4,3,320,128]{4,3,2,1,0:T(8,128)(2,1)}, f32[4096,640]{1,0:T(8,128)}) custom-call(bf16[4096,640]{1,0:T(8,128)(2,1)} %get-tuple-element.96.refs_0_, bf16[4096,640]{1,0:T(8,128)(2,1)} %bitcast.50, s32[1]{0:T(128)} %bitcast.1.refs_1_.refs_2_, bf16[4,3,3,320,128]{4,3,2,1,0:T(8,128)(2,1)} %bitcast.64, ...), custom_call_target="tpu_custom_call", output_to_operand_aliasing={{1}: (5, {})} | custom-call | flops 21474836480 | bytes 31457280 | tf_op jit(solution)/shard_map/mlp_bwd/pallas_call | solution.py:242
  294.2 0.7 reduce-scatter.27.cloned.1.call-update
  294.8 0.2 reduce-scatter.31.cloned.1.call-start
  295.1 33.0 %mlp_bwd.13 = (bf16[2,4,3,320,128]{4,3,2,1,0:T(8,128)(2,1)}, f32[4096,640]{1,0:T(8,128)}) custom-call(bf16[4096,640]{1,0:T(8,128)(2,1)} %get-tuple-element.96.refs_0_, bf16[4096,640]{1,0:T(8,128)(2,1)} %bitcast.51, s32[1]{0:T(128)} %bitcast.1.refs_1_.refs_2_, bf16[4,3,3,320,128]{4,3,2,1,0:T(8,128)(2,1)} %bitcast.65, ...), custom_call_target="tpu_custom_call", output_to_operand_aliasing={{1}: (5, {})} | custom-call | flops 21474836480 | bytes 31457280 | tf_op jit(solution)/shard_map/mlp_bwd/pallas_call | solution.py:242
  328.2 2.5 reduce-scatter.27.cloned.1.call-done
  330.8 34.4 %mlp_bwd.14 = (bf16[2,4,3,320,128]{4,3,2,1,0:T(8,128)(2,1)}, bf16[4096,640]{1,0:T(8,128)(2,1)}) custom-call(bf16[4096,640]{1,0:T(8,128)(2,1)} %get-tuple-element.96.refs_0_, bf16[4096,640]{1,0:T(8,128)(2,1)} %bitcast.52, s32[1]{0:T(128)} %bitcast.1.refs_1_.refs_2_, bf16[4,3,3,320,128]{4,3,2,1,0:T(8,128)(2,1)} %bitcast.66, ...), custom_call_target="tpu_custom_call" | custom-call | flops 21474836480 | bytes 31457280 | tf_op jit(solution)/shard_map/mlp_bwd/pallas_call | solution.py:242
  365.3 7.6 %reduce-scatter.33.cloned.1.call-done = bf16[1,3,320,128]{3,2,1,0:T(8,128)(2,1)} async-done(((bf16[4,3,320,128]{3,2,1,0:T(8,128)(2,1)}), bf16[1,3,320,128]{3,2,1,0:T(8,128)(2,1)}) %reduce-scatter.33.cloned.1.call-update) | async-done | bytes 245776 | tf_op jit(solution)/shard_map/reduce_scatter | solution.py:380
  372.9 0.3 reduce-scatter.41.cloned.1.call-start
  373.1 27.7 %mlp_bwd.15 = (bf16[2,4,3,320,128]{4,3,2,1,0:T(8,128)(2,1)}, f32[4096,640]{1,0:T(8,128)}) custom-call(bf16[4096,640]{1,0:T(8,128)(2,1)} %get-tuple-element.86.refs_0_.refs_1_, bf16[4096,640]{1,0:T(8,128)(2,1)} %get-tuple-element.148.refs_1_, s32[1]{0:T(128)} %bitcast.1.refs_1_.refs_2_, bf16[4,2,3,320,128]{4,3,2,1,0:T(8,128)(2,1)} %bitcast.70, ...), custom_call_target="tpu_custom_call" | custom-call | flops 16106127360 | bytes 48234496 | tf_op jit(solution)/shard_map/mlp_bwd/pallas_call | solution.py:242
  400.8 11.8 %reduce-scatter.37.cloned.1.call-done = bf16[1,3,320,128]{3,2,1,0:T(8,128)(2,1)} async-done(((bf16[4,3,320,128]{3,2,1,0:T(8,128)(2,1)}), bf16[1,3,320,128]{3,2,1,0:T(8,128)(2,1)}) %reduce-scatter.37.cloned.1.call-update) | async-done | bytes 245776 | tf_op jit(solution)/shard_map/reduce_scatter | solution.py:380
  412.7 0.5 reduce-scatter.39.cloned.1.call-update
  413.3 27.7 %mlp_bwd.16 = (bf16[2,4,3,320,128]{4,3,2,1,0:T(8,128)(2,1)}, f32[4096,640]{1,0:T(8,128)}) custom-call(bf16[4096,640]{1,0:T(8,128)(2,1)} %get-tuple-element.86.refs_0_.refs_1_, bf16[4096,640]{1,0:T(8,128)(2,1)} %get-tuple-element.148.refs_1_, s32[1]{0:T(128)} %bitcast.1.refs_1_.refs_2_, ...), custom_call_target="tpu_custom_call", output_to_operand_aliasing={{1}: (7, {})} | custom-call | flops 16106127360 | bytes 48234496 | tf_op jit(solution)/shard_map/mlp_bwd/pallas_call | solution.py:242
  441.1 9.3 %reduce-scatter.39.cloned.1.call-done = bf16[1,4,3,320,128]{4,3,2,1,0:T(8,128)(2,1)} async-done(((bf16[2,4,3,320,128]{4,3,2,1,0:T(8,128)(2,1)}), bf16[1,4,3,320,128]{4,3,2,1,0:T(8,128)(2,1)}) %reduce-scatter.39.cloned.1.call-update) | async-done | bytes 983056 | tf_op jit(solution)/shard_map/reduce_scatter | solution.py:384
  450.5 27.7 %mlp_bwd.17 = (bf16[2,4,3,320,128]{4,3,2,1,0:T(8,128)(2,1)}, f32[4096,640]{1,0:T(8,128)}) custom-call(bf16[4096,640]{1,0:T(8,128)(2,1)} %get-tuple-element.86.refs_0_.refs_1_, bf16[4096,640]{1,0:T(8,128)(2,1)} %get-tuple-element.148.refs_1_, s32[1]{0:T(128)} %bitcast.1.refs_1_.refs_2_, ...), custom_call_target="tpu_custom_call", output_to_operand_aliasing={{1}: (7, {})} | custom-call | flops 16106127360 | bytes 48234496 | tf_op jit(solution)/shard_map/mlp_bwd/pallas_call | solution.py:242
  478.3 14.1 %reduce-scatter.45.cloned.1.call-done = bf16[1,3,320,128]{3,2,1,0:T(8,128)(2,1)} async-done(((bf16[4,3,320,128]{3,2,1,0:T(8,128)(2,1)}), bf16[1,3,320,128]{3,2,1,0:T(8,128)(2,1)}) %reduce-scatter.45.cloned.1.call-update) | async-done | bytes 245776 | tf_op jit(solution)/shard_map/reduce_scatter | solution.py:380
  492.5 0.3 reduce-scatter.53.cloned.1.call-start
  492.8 27.7 %mlp_bwd.18 = (bf16[2,4,3,320,128]{4,3,2,1,0:T(8,128)(2,1)}, f32[4096,640]{1,0:T(8,128)}) custom-call(bf16[4096,640]{1,0:T(8,128)(2,1)} %get-tuple-element.86.refs_0_.refs_1_, bf16[4096,640]{1,0:T(8,128)(2,1)} %get-tuple-element.148.refs_1_, s32[1]{0:T(128)} %bitcast.1.refs_1_.refs_2_, ...), custom_call_target="tpu_custom_call", output_to_operand_aliasing={{1}: (7, {})} | custom-call | flops 16106127360 | bytes 48234496 | tf_op jit(solution)/shard_map/mlp_bwd/pallas_call | solution.py:242
  520.5 0.0 reduce-scatter.57.cloned.1.call-start
  520.6 12.2 %reduce-scatter.49.cloned.1.call-done = bf16[1,3,320,128]{3,2,1,0:T(8,128)(2,1)} async-done(((bf16[4,3,320,128]{3,2,1,0:T(8,128)(2,1)}), bf16[1,3,320,128]{3,2,1,0:T(8,128)(2,1)}) %reduce-scatter.49.cloned.1.call-update) | async-done | bytes 245776 | tf_op jit(solution)/shard_map/reduce_scatter | solution.py:380
  532.8 29.7 %mlp_bwd.19 = (bf16[2,4,3,320,128]{4,3,2,1,0:T(8,128)(2,1)}, bf16[4096,640]{1,0:T(8,128)(2,1)}) custom-call(bf16[4096,640]{1,0:T(8,128)(2,1)} %get-tuple-element.86.refs_0_.refs_1_, bf16[4096,640]{1,0:T(8,128)(2,1)} %get-tuple-element.148.refs_1_, s32[1]{0:T(128)} %bitcast.1.refs_1_.refs_2_, bf16[4,3,3,320,128]{4,3,2,1,0:T(8,128)(2,1)} %bitcast.62, ...), custom_call_target="tpu_custom_call" | custom-call | flops 16106127360 | bytes 48234496 | tf_op jit(solution)/shard_map/mlp_bwd/pallas_call | solution.py:242
  562.6 0.7 reduce-scatter.51.cloned.1.call-update
  563.3 0.7 reduce-scatter.55.cloned.1.call-update
  564.1 6.5 reduce-scatter.57.cloned.1.call-done
  570.6 29.7 %reduce-scatter.51.cloned.1.call-done = bf16[1,3,320,128]{3,2,1,0:T(8,128)(2,1)} async-done(((bf16[4,3,320,128]{3,2,1,0:T(8,128)(2,1)}), bf16[1,3,320,128]{3,2,1,0:T(8,128)(2,1)}) %reduce-scatter.51.cloned.1.call-update) | async-done | bytes 245776 | tf_op jit(solution)/shard_map/reduce_scatter | solution.py:380
  600.3 27.3 %reduce-scatter.55.cloned.1.call-done = bf16[1,3,320,128]{3,2,1,0:T(8,128)(2,1)} async-done(((bf16[4,3,320,128]{3,2,1,0:T(8,128)(2,1)}), bf16[1,3,320,128]{3,2,1,0:T(8,128)(2,1)}) %reduce-scatter.55.cloned.1.call-update) | async-done | bytes 245776 | tf_op jit(solution)/shard_map/reduce_scatter | solution.py:387
  627.7 27.2 %reduce-scatter.59.cloned.1.call-done = bf16[1,3,320,128]{3,2,1,0:T(8,128)(2,1)} async-done(((bf16[4,3,320,128]{3,2,1,0:T(8,128)(2,1)}), bf16[1,3,320,128]{3,2,1,0:T(8,128)(2,1)}) %reduce-scatter.59.cloned.1.call-update) | async-done | bytes 245776 | tf_op jit(solution)/shard_map/reduce_scatter | solution.py:387
  654.9 4.1 unpack.1
  (49 shorter events, 1.1 us)
Async XLA Ops:
  7.2 49.6 %all-gather.9.cloned.1.call-start = ((), (), s32[]{:S(2)}) async-start(), calls=%async_computation.40 | async-start | bytes 2457600 | tf_op jit(solution)/shard_map/all_gather | solution.py:330
  10.8 106.8 %all-gather.11.cloned.1.call-start = ((), (), s32[]{:S(2)}) async-start(), calls=%async_computation.41 | async-start | bytes 3686400 | tf_op jit(solution)/shard_map/all_gather | solution.py:330
  11.5 152.5 %all-gather.13.cloned.1.call-start = ((), (), s32[]{:S(2)}) async-start(), calls=%async_computation.42 | async-start | bytes 2457600 | tf_op jit(solution)/shard_map/all_gather | solution.py:330
  56.8 3.9 collective-permute-start
  56.8 165.5 %all-gather.15.cloned.1.call-start = ((), (), s32[]{:S(2)}) async-start(), calls=%async_computation.43 | async-start | bytes 3686400 | tf_op jit(solution)/shard_map/all_gather | solution.py:330
  117.6 5.3 collective-permute-start.1
  117.6 137.8 %reduce-scatter.21.cloned.1.call-start = ((), (), s32[]{:S(2)}) async-start(), calls=%async_computation.20 | async-start | bytes 2949120 | tf_op jit(solution)/shard_map/reduce_scatter | solution.py:384
  164.0 23.5 %collective-permute-start.2 = (bf16[4,2,3,320,128]{4,3,2,1,0:T(8,128)(2,1)}, bf16[4,2,3,320,128]{4,3,2,1,0:T(8,128)(2,1)}, u32[]{:S(2)}, u32[]{:S(2)}) collective-permute-start(bf16[4,2,3,320,128]{4,3,2,1,0:T(8,128)(2,1)} %bitcast.72), channel_id=1, source_target_pairs={{0,1},{1,0},{2,3},{3,2},{4,5},{5,4},{6,7},{7,6},{8,9},{9,8},{10,11... | collective-permute-start | bytes 5898248 | tf_op jit(solution)/shard_map/ppermute | solution.py:340
  219.6 74.5 %reduce-scatter.23.cloned.1.call-start = ((), (), s32[]{:S(2)}) async-start(), calls=%async_computation.21 | async-start | bytes 2949120 | tf_op jit(solution)/shard_map/reduce_scatter | solution.py:384
  255.3 38.8 %reduce-scatter.25.cloned.1.call-start = ((), (), s32[]{:S(2)}) async-start(), calls=%async_computation.22 | async-start | bytes 1228800 | tf_op jit(solution)/shard_map/reduce_scatter | solution.py:380
  255.3 5.8 collective-permute-start.3
  256.0 72.2 %reduce-scatter.29.cloned.1.call-start = ((), (), s32[]{:S(2)}) async-start(), calls=%async_computation.24 | async-start | bytes 1228800 | tf_op jit(solution)/shard_map/reduce_scatter | solution.py:380
  294.1 36.6 %reduce-scatter.27.cloned.1.call-start = ((), (), s32[]{:S(2)}) async-start(), calls=%async_computation.23 | async-start | bytes 2949120 | tf_op jit(solution)/shard_map/reduce_scatter | solution.py:384
  294.8 70.4 %reduce-scatter.31.cloned.1.call-start = ((), (), s32[]{:S(2)}) async-start(), calls=%async_computation.25 | async-start | bytes 2949120 | tf_op jit(solution)/shard_map/reduce_scatter | solution.py:384
  328.1 44.7 %reduce-scatter.33.cloned.1.call-start = ((), (), s32[]{:S(2)}) async-start(), calls=%async_computation.26 | async-start | bytes 1228800 | tf_op jit(solution)/shard_map/reduce_scatter | solution.py:380
  330.7 70.1 %reduce-scatter.35.cloned.1.call-start = ((), (), s32[]{:S(2)}) async-start(), calls=%async_computation.27 | async-start | bytes 2949120 | tf_op jit(solution)/shard_map/reduce_scatter | solution.py:384
  365.2 47.4 %reduce-scatter.37.cloned.1.call-start = ((), (), s32[]{:S(2)}) async-start(), calls=%async_computation.28 | async-start | bytes 1228800 | tf_op jit(solution)/shard_map/reduce_scatter | solution.py:380
  372.9 68.2 %reduce-scatter.41.cloned.1.call-start = ((), (), s32[]{:S(2)}) async-start(), calls=%async_computation.30 | async-start | bytes 1228800 | tf_op jit(solution)/shard_map/reduce_scatter | solution.py:380
  412.6 37.8 %reduce-scatter.39.cloned.1.call-start = ((), (), s32[]{:S(2)}) async-start(), calls=%async_computation.29 | async-start | bytes 2949120 | tf_op jit(solution)/shard_map/reduce_scatter | solution.py:384
  413.2 65.1 %reduce-scatter.43.cloned.1.call-start = ((), (), s32[]{:S(2)}) async-start(), calls=%async_computation.31 | async-start | bytes 2949120 | tf_op jit(solution)/shard_map/reduce_scatter | solution.py:384
  441.0 51.4 %reduce-scatter.45.cloned.1.call-start = ((), (), s32[]{:S(2)}) async-start(), calls=%async_computation.32 | async-start | bytes 1228800 | tf_op jit(solution)/shard_map/reduce_scatter | solution.py:380
  450.4 70.1 %reduce-scatter.47.cloned.1.call-start = ((), (), s32[]{:S(2)}) async-start(), calls=%async_computation.33 | async-start | bytes 2949120 | tf_op jit(solution)/shard_map/reduce_scatter | solution.py:384
  478.2 54.5 %reduce-scatter.49.cloned.1.call-start = ((), (), s32[]{:S(2)}) async-start(), calls=%async_computation.34 | async-start | bytes 1228800 | tf_op jit(solution)/shard_map/reduce_scatter | solution.py:380
  492.5 70.9 %reduce-scatter.53.cloned.1.call-start = ((), (), s32[]{:S(2)}) async-start(), calls=%async_computation.36 | async-start | bytes 2949120 | tf_op jit(solution)/shard_map/reduce_scatter | solution.py:384
  520.5 50.1 %reduce-scatter.57.cloned.1.call-start = ((), (), s32[]{:S(2)}) async-start(), calls=%async_computation.38 | async-start | bytes 2949120 | tf_op jit(solution)/shard_map/reduce_scatter | solution.py:384
  562.5 37.8 %reduce-scatter.51.cloned.1.call-start = ((), (), s32[]{:S(2)}) async-start(), calls=%async_computation.35 | async-start | bytes 1228800 | tf_op jit(solution)/shard_map/reduce_scatter | solution.py:380
  563.3 64.4 %reduce-scatter.55.cloned.1.call-start = ((), (), s32[]{:S(2)}) async-start(), calls=%async_computation.37 | async-start | bytes 1228800 | tf_op jit(solution)/shard_map/reduce_scatter | solution.py:387
  564.0 90.9 %reduce-scatter.59.cloned.1.call-start = ((), (), s32[]{:S(2)}) async-start(), calls=%async_computation.39 | async-start | bytes 1228800 | tf_op jit(solution)/shard_map/reduce_scatter | solution.py:387
Sparse Core Ops, SparseCore 0:
  10.9 45.8 all-gather.8
  58.9 58.5 all-gather.10
  119.7 41.9 all-gather.12
  163.7 58.5 all-gather.14
  224.4 8.0 reduce-scatter.20
  255.4 8.3 reduce-scatter.22
  266.1 26.9 reduce-scatter.24
  295.5 24.9 reduce-scatter.28
  322.8 7.8 reduce-scatter.26
  332.8 10.2 reduce-scatter.30
  345.4 27.3 reduce-scatter.32
  375.0 7.8 reduce-scatter.34
  385.2 27.3 reduce-scatter.36
  414.8 24.9 reduce-scatter.40
  442.5 7.8 reduce-scatter.38
  452.5 10.2 reduce-scatter.42
  465.0 27.3 reduce-scatter.44
  495.1 7.8 reduce-scatter.46
  505.4 27.3 reduce-scatter.48
  534.9 7.8 reduce-scatter.52
  562.6 7.8 reduce-scatter.56
  572.9 27.3 reduce-scatter.50
  602.7 24.9 reduce-scatter.54
  629.8 24.9 reduce-scatter.58
